TPU v7x, 32 devices: a whole 2x2x4 slice. The times are simulated.
32 devices in a mesh: dom: 16 (over z, x, core), rep: 2 (over y).
Axes of the slice: x: 2, y: 2, z: 4, core: 2. Of those that a mesh axis runs over, the one named last changes fastest.
Arguments:
- node_feats: bfloat16 [12288, 256], P(('dom', 'rep')), may hold values from -6 to 6
- node_ids: int32 [12288], replicated, may hold values from 0 to 16777215
- tile_row: int32 [16, 2, 16], replicated, may hold values from -1 to 95, as said below
- tile_col: int32 [16, 2, 16], replicated, may hold values from -1 to 95, as said below
- tile_count: int32 [16, 2, 16], replicated, may hold values from 1 to 128, as said below
- self_weight: bfloat16 [256, 512], replicated, may hold values from -0.375 to 0.375
- neigh_weight: bfloat16 [256, 512], replicated, may hold values from -3 to 3
- out_grad: bfloat16 [12288, 512], P(('dom', 'rep')), may hold values from -6 to 6
Outputs:
- hidden_out: bfloat16 [12288, 512], P(('dom', 'rep'))
- feat_grad: bfloat16 [12288, 256], P(('dom', 'rep'))
- self_grad: float32 [256, 512], replicated
- neigh_grad: float32 [256, 512], replicated
Inputs may be any that keep to these rules, and one draw needn't show every extreme that they name: `tile_row`: entry [d, r, s] is -1 where the slot holds no tile, else a block row of dom group d: d * 6 plus 0 to 5. In every draw some pair (d, r) has all 16 of its slots filled. `tile_col`: -1 exactly where tile_row is -1; else one of the blocks of device (s, r): s * 6 + r * 3 plus 0 to 2. `tile_count`: read only where a tile is present.
All inputs are finite; a program needn't handle non-finite values.
Results may differ from a plain program's by a relative error of at most 0.01.
Values may be sent and summed in bfloat16 or wider, within the bound.
A program may use at most 64 MiB of HBM per device.

v0:
```python
import functools
import math

import jax
import jax.numpy as jnp
from jax import lax
from jax.experimental import pallas as pl
from jax.experimental.pallas import tpu as pltpu
from jax.sharding import PartitionSpec as P

TILE = 128

MESH = pl.DeviceIdType.MESH
OVER_ROWS = (((0,), (0,)), ((), ()))
OVER_COLS = (((1,), (1,)), ((), ()))


def greet(devices):
    barrier = pltpu.get_barrier_semaphore()
    for device in devices:
        pl.semaphore_signal(barrier, inc=1, device_id=device, device_id_type=MESH)
    pl.semaphore_wait(barrier, len(devices))


def send(src, dst, sems, slot, device):
    copy = pltpu.make_async_remote_copy(
        src_ref=src,
        dst_ref=dst,
        send_sem=sems.at[0, slot],
        recv_sem=sems.at[1, slot],
        device_id=device,
        device_id_type=MESH,
    )
    copy.start()
    return copy


def dense(
    rep_total, partials, divisor, feats, w_self, w_neigh, cotangent,
    hidden, terms, back, gathered, landed, mine, sems_in, sems_out,
):
    dom, me = lax.axis_index("dom"), lax.axis_index("rep")
    peers = [lax.rem(me + k, rep_total) for k in range(1, rep_total)]
    greet([(dom, peer) for peer in peers])
    copies = [
        send(partials.at[peer], landed.at[k], sems_in, k, (dom, peer))
        for k, peer in enumerate(peers)
    ]
    x = feats[...]
    preact = jnp.dot(x, w_self[...], preferred_element_type=jnp.float32)
    summed = partials[me].astype(jnp.float32)
    for k, copy in enumerate(copies):
        copy.wait()
        summed = summed + landed[k].astype(jnp.float32)
    div = divisor[...]
    mean = (summed / div).astype(jnp.bfloat16)
    preact = preact + jnp.dot(mean, w_neigh[...], preferred_element_type=jnp.float32)
    logistic = jax.nn.sigmoid(preact)
    grad = (
        cotangent[...].astype(jnp.float32) * logistic * (1.0 + preact * (1.0 - logistic))
    ).astype(jnp.bfloat16)
    spread = lax.dot_general(grad, w_neigh[...], OVER_COLS, preferred_element_type=jnp.float32)
    mine[...] = (spread / div).astype(jnp.bfloat16)
    copies = [
        send(mine, gathered.at[me], sems_out, k, (dom, peer)) for k, peer in enumerate(peers)
    ]
    gathered[me] = mine[...]
    hidden[...] = (preact * logistic).astype(jnp.bfloat16)
    terms[0] = lax.dot_general(
        x, grad, OVER_ROWS, preferred_element_type=jnp.float32
    ).astype(jnp.bfloat16)
    terms[1] = lax.dot_general(
        mean, grad, OVER_ROWS, preferred_element_type=jnp.float32
    ).astype(jnp.bfloat16)
    back[...] = lax.dot_general(grad, w_self[...], OVER_COLS, preferred_element_type=jnp.float32)
    for copy in copies:
        copy.wait()


def finish(
    dom_total, rep_total, inner, scale, terms, grads,
    landed, share, strips, final, sems_a, sems_b, sems_c, sems_d,
):
    dom, rep = lax.axis_index("dom"), lax.axis_index("rep")
    outer = dom_total // inner
    plane = inner * rep_total
    layer, within = dom // inner, lax.rem(dom, inner)
    spot = within * rep_total + rep
    plane_peers = []
    for k in range(1, plane):
        other = lax.rem(spot + k, plane)
        plane_peers.append(
            (other, (layer * inner + other // rep_total, lax.rem(other, rep_total)))
        )
    layer_peers = []
    for k in range(1, outer):
        other = lax.rem(layer + k, outer)
        layer_peers.append((other, (other * inner + within, rep)))
    greet([device for _, device in plane_peers + layer_peers])
    first = [
        send(terms.at[other], landed.at[k], sems_a, k, device)
        for k, (other, device) in enumerate(plane_peers)
    ]
    total = terms[spot].astype(jnp.float32)
    for k, copy in enumerate(first):
        copy.wait()
        total = total + landed[k].astype(jnp.float32)
    share[...] = total.astype(jnp.bfloat16)
    second = [
        send(share.at[other], strips.at[k], sems_b, k, device)
        for k, (other, device) in enumerate(layer_peers)
    ]
    total = share[layer].astype(jnp.float32)
    for k, copy in enumerate(second):
        copy.wait()
        total = total + strips[k].astype(jnp.float32)
    final[...] = (total * scale).astype(jnp.bfloat16)
    third = [
        send(final, grads.at[spot, layer], sems_c, k, device)
        for k, (_, device) in enumerate(layer_peers)
    ]
    grads[spot, layer] = final[...]
    for copy in third:
        copy.wait()
    fourth = [
        send(grads.at[spot], grads.at[spot], sems_d, k, device)
        for k, (_, device) in enumerate(plane_peers)
    ]
    for copy in fourth:
        copy.wait()


def pair_sems(count):
    return pltpu.SemaphoreType.DMA((2, max(count, 1)))


def call(kernel, out_shapes, scratch, ident, *operands):
    return pl.pallas_call(
        kernel,
        out_shape=out_shapes,
        in_specs=[pl.BlockSpec(memory_space=pltpu.VMEM)] * len(operands),
        out_specs=jax.tree.map(lambda _: pl.BlockSpec(memory_space=pltpu.VMEM), out_shapes),
        scratch_shapes=scratch,
        compiler_params=pltpu.CompilerParams(collective_id=ident, has_side_effects=True),
        cost_estimate=pl.CostEstimate(
            flops=8_000_000_000, bytes_accessed=4_000_000, transcendentals=0
        ),
    )(*operands)


def edge_masks(row_ids, col_ids, limits, tile_size):
    left_ids = (row_ids % 4093)[:, :, None]
    right_ids = (col_ids % 4091)[:, None, :]
    hashed = (left_ids * right_ids + left_ids + 3 * right_ids) % 4099 % tile_size
    return (hashed < limits[:, None, None]).astype(jnp.bfloat16)


def shards(
    node_feats, node_ids, tile_row, tile_col, tile_count, self_weight, neigh_weight, out_grad
):
    dom_total = lax.axis_size("dom")
    rep_total = lax.axis_size("rep")
    dom_here = lax.axis_index("dom")
    rep_here = lax.axis_index("rep")
    rows_here, width_in = node_feats.shape
    blocks_here = rows_here // TILE
    group_blocks = blocks_here * rep_total
    id_blocks = node_ids.reshape(-1, TILE)
    group_first = dom_here * group_blocks
    own_first = group_first + rep_here * blocks_here
    inbound_rows = tile_row[dom_here, rep_here]
    inbound_present = inbound_rows >= 0
    inbound_block = jnp.where(inbound_present, inbound_rows, 0)
    inbound_cols = jnp.where(inbound_present, tile_col[dom_here, rep_here], 0)
    inbound_limits = jnp.where(inbound_present, tile_count[dom_here, rep_here], 0)
    inbound_masks = edge_masks(
        id_blocks[inbound_block], id_blocks[inbound_cols], inbound_limits, TILE
    )
    inbound_offset = jnp.where(inbound_present, inbound_block - group_first, 0)
    row_select = (
        (jnp.arange(group_blocks)[:, None] == inbound_offset[None, :]) & inbound_present[None, :]
    ).astype(jnp.float32)
    outbound_cols = tile_col[:, rep_here, dom_here]
    outbound_present = outbound_cols >= 0
    outbound_offset = jnp.where(outbound_present, outbound_cols - own_first, 0)
    own_select = (
        (outbound_offset[:, None] == jnp.arange(blocks_here)[None, :]) & outbound_present[:, None]
    ).astype(jnp.float32)
    feat_blocks = node_feats.reshape(blocks_here, TILE, width_in)
    outgoing = feat_blocks[outbound_offset]
    products = jnp.einsum(
        "sij,sjf->sif",
        inbound_masks,
        lax.all_to_all(outgoing, "dom", split_axis=0, concat_axis=0, tiled=True),
        preferred_element_type=jnp.float32,
    )
    partial_value = jnp.einsum("bs,sif->bif", row_select, products)
    group_rows = tile_row[dom_here].reshape(-1)
    group_limits = tile_count[dom_here].reshape(-1)
    owned_rows = group_rows[:, None] == own_first + jnp.arange(blocks_here)[None, :]
    degree = jnp.sum(jnp.where(owned_rows, group_limits[:, None], 0), axis=0).astype(jnp.float32)
    divisor = jnp.repeat(jnp.maximum(degree, 1.0), TILE)[:, None]
    width_out = self_weight.shape[1]
    hidden_out, both_terms, self_back, group_spread = call(
        functools.partial(dense, rep_total),
        (
            jax.ShapeDtypeStruct((rows_here, width_out), jnp.bfloat16),
            jax.ShapeDtypeStruct((2, width_in, width_out), jnp.bfloat16),
            jax.ShapeDtypeStruct((rows_here, width_in), jnp.float32),
            jax.ShapeDtypeStruct((rep_total, rows_here, width_in), jnp.bfloat16),
        ),
        [
            pltpu.VMEM((max(rep_total - 1, 1), rows_here, width_in), jnp.bfloat16),
            pltpu.VMEM((rows_here, width_in), jnp.bfloat16),
            pair_sems(rep_total - 1),
            pair_sems(rep_total - 1),
        ],
        1,
        partial_value.reshape(rep_total, rows_here, width_in).astype(jnp.bfloat16),
        divisor,
        node_feats,
        self_weight,
        neigh_weight,
        out_grad,
    )
    group_spread = group_spread.reshape(group_blocks, TILE, width_in)
    grad_scale = 1.0 / math.sqrt(rows_here * dom_total * rep_total)
    picked_rows = group_spread[inbound_offset]
    products = jnp.einsum(
        "sij,sif->sjf", inbound_masks, picked_rows, preferred_element_type=jnp.float32
    )
    inner = math.gcd(dom_total, 4)
    outer = dom_total // inner
    plane = inner * rep_total
    strip = 2 * width_in // (dom_total * rep_total)
    returned = lax.all_to_all(
        products.astype(jnp.bfloat16), "dom", split_axis=0, concat_axis=0, tiled=True
    )
    both_grads = call(
        functools.partial(finish, dom_total, rep_total, inner, grad_scale),
        jax.ShapeDtypeStruct((plane, outer, strip, width_out), jnp.bfloat16),
        [
            pltpu.VMEM((max(plane - 1, 1), outer, strip, width_out), jnp.bfloat16),
            pltpu.VMEM((outer, strip, width_out), jnp.bfloat16),
            pltpu.VMEM((max(outer - 1, 1), strip, width_out), jnp.bfloat16),
            pltpu.VMEM((strip, width_out), jnp.bfloat16),
            pair_sems(plane - 1),
            pair_sems(outer - 1),
            pair_sems(outer - 1),
            pair_sems(plane - 1),
        ],
        2,
        both_terms.reshape(plane, outer, strip, width_out),
    )
    both_grads = both_grads.reshape(2, width_in, width_out).astype(jnp.float32)
    returned = returned.astype(jnp.float32)
    transposed = jnp.einsum("db,djf->bjf", own_select, returned)
    feat_grad = (self_back + transposed.reshape(rows_here, width_in)).astype(jnp.bfloat16)
    return (hidden_out, feat_grad, both_grads[0], both_grads[1])


def solution(mesh):
    placed = (P(("dom", "rep"), None), P(), P(), P(), P(), P(), P(), P(("dom", "rep"), None))
    return jax.shard_map(
        shards,
        mesh=mesh,
        in_specs=placed,
        out_specs=(P(("dom", "rep"), None), P(("dom", "rep"), None), P(), P()),
        check_vma=False,
    )
```

profile of v0, /device:TPU:0, one launch (start us, length us, event | category | flops | bytes accessed | tf_op | source)
XLA Modules:
  0.0 109.8 jit_solution(1526797325534571998)
XLA Ops:
  0.6 0.0 copy-start
  0.7 0.7 fusion.36
  1.3 1.4 %subtract_reduce_fusion = (s32[16]{0:T(128)S(1)}, s32[16]{0:T(128)S(1)}) fusion(s32[]{:T(128)S(6)} %add.127, s32[16,2,16]{2,1,0:T(2,128)} %param.11, s32[]{:T(128)S(6)} %select_n.163, s32[]{:T(128)S(6)} %select_n.162), kind=kLoop, calls=%fused_computation.28 | loop fusion | flops 48 | bytes 204 | tf_op jit(solution)/shard_map/sub | solution.py:185
  2.8 0.7 fusion.32
  3.5 2.5 %gather_fusion.2 = bf16[16,128,256]{2,1,0:T(8,128)(2,1)} fusion(bf16[3,128,256]{2,1,0:T(8,128)(2,1)} %bitcast.71, s32[1024]{0:T(1024)S(1)} %pad_clamp_fusion.1), kind=kCustom, calls=%fused_computation.2 | custom fusion | bytes 2097216 | tf_op jit(solution)/shard_map/gather | solution.py:190
  6.0 7.4 %all-to-all-start = ((bf16[16,128,256]{2,1,0:T(8,128)(2,1)}), bf16[16,128,256]{2,1,0:T(8,128)(2,1)S(1)}, u32[]{:S(2)}, u32[]{:S(2)}) async-start(bf16[16,128,256]{2,1,0:T(8,128)(2,1)} %gather_fusion.2), calls=%async_computation | async-start | bytes 2097152 | tf_op jit(solution)/shard_map/all_to_all | solution.py:194
  13.4 0.0 copy-done
  13.4 0.6 gather_fusion.1
  14.0 0.6 gather_fusion
  14.6 0.7 constant_dynamic-slice_fusion
  15.3 0.1 broadcast_in_dim.18
  15.4 0.1 eq.50
  15.4 0.2 select_reduce_fusion
  15.6 0.1 broadcast_bitcast_fusion
  15.7 0.8 copy.31
  16.6 0.7 fusion.35
  17.3 19.0 %all-to-all-done = bf16[16,128,256]{2,1,0:T(8,128)(2,1)S(1)} async-done(((bf16[16,128,256]{2,1,0:T(8,128)(2,1)}), bf16[16,128,256]{2,1,0:T(8,128)(2,1)S(1)}, u32[]{:S(2)}, u32[]{:S(2)}) %all-to-all-start) | async-done | bytes 1048608 | tf_op jit(solution)/shard_map/all_to_all | solution.py:194
  36.3 2.2 %fusion.14 = bf16[16,128,256]{2,1,0:T(8,128)(2,1)S(1)} fusion(bf16[16,128,256]{2,1,0:T(8,128)(2,1)S(1)} %all-to-all-done, s32[16]{0:T(128)S(1)} %get-tuple-element.21, s32[16,128]{1,0:T(8,128)S(1)} %get-tuple-element.19, s32[16,128]{1,0:T(8,128)S(1)} %get-tuple-element.18, s32[16,128]{1,0:T(8,128)S(1)} %add_select_fusion.3), kind=kOutput, calls=%fused_computation.22 | convolution fusion | flops 139722752 | bytes 2121792 | tf_op jit(solution)/shard_map/sij,sjf->sif/dot_general | solution.py:191
  38.5 0.7 fusion.2
  39.2 0.8 copy.25
  40.0 17.3 %shard_map.111 = (bf16[384,512]{1,0:T(8,128)(2,1)}, bf16[2,256,512]{2,1,0:T(8,128)(2,1)}, f32[384,256]{1,0:T(8,128)}, bf16[2,384,256]{2,1,0:T(8,128)(2,1)}) custom-call(bf16[2,384,256]{2,1,0:T(8,128)(2,1)} %bitcast.75, f32[384,1]{1,0:T(8,128)} %bitcast.76, bf16[384,256]{1,0:T(8,128)(2,1)} %feats.1, bf16[256,512]{1,0:T(8,128)(2,1)} %w_self.1, ...), custom_call_target="tpu_custom_call" | custom-call | flops 8000000000 | bytes 4000000 | tf_op jit(solution)/shard_map/pallas_call | solution.py:138
  57.3 1.6 %gather_fusion.3 = bf16[16,128,256]{2,1,0:T(8,128)(2,1)S(1)} fusion(bf16[6,128,256]{2,1,0:T(8,128)(2,1)} %bitcast.72, s32[1024]{0:T(1024)S(1)} %pad_clamp_fusion), kind=kCustom, calls=%fused_computation.3 | custom fusion | bytes 2097216 | tf_op jit(solution)/shard_map/gather | solution.py:228
  58.9 2.9 %convolution_convert_fusion = bf16[16,128,256]{2,1,0:T(8,128)(2,1)} fusion(bf16[16,128,256]{2,1,0:T(8,128)(2,1)S(1)} %gather_fusion.3, s32[16]{0:T(128)S(1)} %get-tuple-element.21, s32[16,128]{1,0:T(8,128)S(1)} %get-tuple-element.19, s32[16,128]{1,0:T(8,128)S(1)} %get-tuple-element.18, s32[16,128]{1,0:T(8,128)S(1)} %add_select_fusion.3), kind=kOutput, calls=%fused_computation.10 | convolution fusion | flops 140247040 | bytes 2121792 | tf_op jit(solution)/shard_map/sij,sif->sjf/dot_general | solution.py:229
  61.8 0.0 copy-start.3
  61.8 6.3 %all-to-all-start.1 = ((bf16[16,128,256]{2,1,0:T(8,128)(2,1)}), bf16[16,128,256]{2,1,0:T(8,128)(2,1)S(1)}, u32[]{:S(2)}, u32[]{:S(2)}) async-start(bf16[16,128,256]{2,1,0:T(8,128)(2,1)} %convolution_convert_fusion), calls=%async_computation.1 | async-start | bytes 2097152 | tf_op jit(solution)/shard_map/all_to_all | solution.py:236
  68.1 0.0 copy-done.3
  68.1 0.5 compare_reduce_fusion
  68.6 36.6 %shard_map.112 = bf16[8,4,16,512]{3,2,1,0:T(8,128)(2,1)} custom-call(bf16[8,4,16,512]{3,2,1,0:T(8,128)(2,1)} %bitcast.78), custom_call_target="tpu_custom_call" | custom-call | flops 8000000000 | bytes 4000000 | tf_op jit(solution)/shard_map/pallas_call | solution.py:138
  105.2 2.1 %fusion.44 = (f32[4,4,16,512]{3,2,1,0:T(8,128)}, f32[4,4,16,512]{3,2,1,0:T(8,128)}) fusion(bf16[8,4,16,512]{3,2,1,0:T(8,128)(2,1)} %shard_map.112), kind=kLoop, calls=%fused_computation.82 | loop fusion | bytes 2097152 | tf_op jit(solution)/shard_map/slice | solution.py:259
  107.3 0.0 copy-start.2
  107.3 0.0 all-to-all-done.1
  107.4 0.7 fusion.7
  108.0 0.0 copy-start.1
  108.0 0.1 copy.28
  108.1 0.2 copy-done.2
  108.3 0.7 fusion.12
  109.1 0.0 copy-done.1
  109.1 0.7 copy.41
  (11 shorter events, 0.1 us)
Async XLA Ops:
  0.6 12.8 %copy-start = (s32[12288]{0:T(1024)S(1)}, s32[12288]{0:T(1024)}, u32[]{:S(2)}) copy-start(s32[12288]{0:T(1024)} %param.9) | copy-start | bytes 147460
  6.0 30.3 %all-to-all-start = ((bf16[16,128,256]{2,1,0:T(8,128)(2,1)}), bf16[16,128,256]{2,1,0:T(8,128)(2,1)S(1)}, u32[]{:S(2)}, u32[]{:S(2)}) async-start(bf16[16,128,256]{2,1,0:T(8,128)(2,1)} %gather_fusion.2), calls=%async_computation | async-start | bytes 2097152 | tf_op jit(solution)/shard_map/all_to_all | solution.py:194
  61.8 6.3 %copy-start.3 = (s32[16,2,16]{2,1,0:T(2,128)S(1)}, s32[16,2,16]{2,1,0:T(2,128)}, u32[]{:S(2)}) copy-start(s32[16,2,16]{2,1,0:T(2,128)} %param.11) | copy-start | bytes 6148
  61.8 45.5 %all-to-all-start.1 = ((bf16[16,128,256]{2,1,0:T(8,128)(2,1)}), bf16[16,128,256]{2,1,0:T(8,128)(2,1)S(1)}, u32[]{:S(2)}, u32[]{:S(2)}) async-start(bf16[16,128,256]{2,1,0:T(8,128)(2,1)} %convolution_convert_fusion), calls=%async_computation.1 | async-start | bytes 2097152 | tf_op jit(solution)/shard_map/all_to_all | solution.py:236
  107.3 1.0 copy-start.2
  108.0 1.0 copy-start.1
where the time goes:
time: 111 us; the launch traced here: 110 us
  Pallas kernels  53.9 us (49%)
  waiting for transfers between devices  19 us (17%)
  starting transfers between devices  13.7 us (12%)
  local copies, waits for them, and re-layouts  11 us (10%)
  matrix products  6.44 us (6%)
  other arithmetic  4.96 us (4%)
    pallas_call x2, Pallas kernels, call(): pl.pallas_call(kernel, out_shape=out_shapes, in_specs=[pl.BlockSpec(memor...  53.9 us
    all_to_all x1, waiting for transfers between devices, shards(): lax.all_to_all(outgoing, 'dom', split_axis=0, concat_axis=0, tiled=True)  19 us
    all_to_all x1, starting transfers between devices, shards(): lax.all_to_all(outgoing, 'dom', split_axis=0, concat_axis=0, tiled=True)  7.39 us
    all_to_all x1, starting transfers between devices, shards(): lax.all_to_all(products.astype(jnp.bfloat16), 'dom', split_axis=0, concat...  6.3 us
    dot_general x1, matrix products, shards(): jnp.einsum('sij,sif->sjf', inbound_masks, picked_rows, preferred_element_...  2.87 us
    gather x1, local copies, waits for them, and re-layouts, shards(): outgoing = feat_blocks[outbound_offset]  2.51 us
    dot_general x1, matrix products, shards(): jnp.einsum('sij,sjf->sif', inbound_masks, lax.all_to_all(outgoing, 'dom',...  2.23 us
  transfers between devices with their start and end apart: 2, of which 1 were waited for; matrix products, arithmetic and copies ran while one was open for 6% of the time, Pallas kernels for 33%

commit v1 on v0

v1 whole, which is shorter than its diff:
```python
import functools
import math

import jax
import jax.numpy as jnp
from jax import lax
from jax.experimental import pallas as pl
from jax.experimental.pallas import tpu as pltpu
from jax.sharding import PartitionSpec as P

TILE = 128
LANES = 128
HASH = 4099.0

MESH = pl.DeviceIdType.MESH
OVER_ROWS = (((0,), (0,)), ((), ()))
OVER_COLS = (((1,), (1,)), ((), ()))
BF16 = jnp.bfloat16
F32 = jnp.float32


def modulo(value, base):
    quotient = jnp.floor(value * ((1.0 - 2.0**-20) / base))
    left = value - quotient * base
    return jnp.where(left >= base, left - base, left)


def across(row):
    return jnp.broadcast_to(row, (TILE, TILE)).T


def bucket(hashed):
    left = modulo(hashed, HASH)
    return left - jnp.floor(left * (1.0 / TILE)) * TILE


class Plan:
    def __init__(self, dom_total, rep_total, rows, width_in, width_out):
        self.line = math.gcd(dom_total, 4)
        self.plane = dom_total // self.line
        self.cores = math.gcd(self.plane, 2)
        self.cols = self.plane // self.cores
        self.reps = rep_total
        self.doms = dom_total
        self.own = rows // TILE
        self.group = self.own * rep_total
        self.halves = width_in // LANES
        self.width_in, self.width_out = width_in, width_out
        self.ring = self.cols * rep_total
        self.strip = 2 * width_in // (self.cores * self.ring * self.line)
        self.split = self.strip % 16 == 0
        self.ahead = self.line * self.group * self.plane * TILE * TILE * 2 <= 2**23


def fused(plan, scale, *refs):
    refs = list(refs)

    def take(count):
        out, refs[:count] = refs[:count], []
        return out

    line, plane, reps, own, group, halves = (
        plan.line, plan.plane, plan.reps, plan.own, plan.group, plan.halves,
    )
    tile_row, tile_col, tile_count, ids, x, cot, w_self, w_neigh = take(8)
    hidden, feat_grad, grads = take(3)
    left_ids, right_ids, wide, tall = take(4)
    held, chosen, picked, total, partial, landed, mean, preact, back = take(9)
    spread = take(halves)
    picked_back, chosen_back, sums_out, sums_in = take(4)
    if plan.split:
        terms, first_in, first, second_in, second, third_in, final = take(7)
    line_sems, pick_sems, rep_sems, spread_sems, pick_back_sems, sum_sems = take(6)
    if plan.split:
        core_sems, ring_sems, far_sems, far_back_sems, ring_back_sems, core_back_sems = take(6)

    dom, rep = lax.axis_index("dom"), lax.axis_index("rep")
    z, p = dom // plane, lax.rem(dom, plane)

    def device(zz, pp, rr):
        return (zz * plane + pp, rr)

    def remote(src, dst, sems, index, target):
        return pltpu.make_async_remote_copy(
            src_ref=src,
            dst_ref=dst,
            send_sem=sems.at[(0,) + index],
            recv_sem=sems.at[(1,) + index],
            device_id=target,
            device_id_type=MESH,
        )

    line_peers = [lax.rem(z + k, line) for k in range(1, line)]
    plane_peers = [lax.rem(p + k, plane) for k in range(1, plane)]
    rep_peers = [lax.rem(rep + k, reps) for k in range(1, reps)]
    col, core = p // plan.cores, lax.rem(p, plan.cores)

    everyone = [device(other, p, rep) for other in line_peers]
    everyone += [device(z, other, rep) for other in plane_peers]
    for k in range(plan.cols):
        other = lax.rem(col + k, plan.cols) * plan.cores + core
        everyone += [device(z, other, peer) for peer in rep_peers]
    barrier = pltpu.get_barrier_semaphore()
    for peer in everyone:
        pl.semaphore_signal(barrier, inc=1, device_id=peer, device_id_type=MESH)

    node = ids[...].astype(F32)
    left_ids[...] = modulo(node, 4093.0)
    right_ids[...] = modulo(node, 4091.0)

    home = line - 1
    levels = [[(above, k) for above in range(2)] for k in range(1, line)]

    def slot_of(above, k):
        return line - 1 - k if above else k - 1

    def spot(above, k):
        return z + k if above else z - k

    def exists(above, k):
        return z < line - k if above else z >= k

    def half(h):
        return slice(h * LANES, (h + 1) * LANES)

    def passes_on(above):
        return z >= 1 if above else z < line - 1

    def line_copy(h, above, k):
        slot = slot_of(above, k + 1)
        src = held.at[h, slot_of(above, k)] if k else x.at[:, :, half(h)]
        return remote(
            src, held.at[h, slot], line_sems, (above, h, k), device(z + 1 - 2 * above, p, rep)
        )

    pl.semaphore_wait(barrier, len(everyone))

    def choose(h, slot, source, blocks):
        first_own = ((source * plane + p) * reps + rep) * own

        def block_for(d):
            offset = tile_col[d, rep, source * plane + p] - first_own
            value = blocks[0]
            for b in range(1, own):
                value = lax.select(offset == b, blocks[b], value)
            return value

        for k, peer in enumerate(plane_peers):
            chosen[h, slot, k] = block_for(z * plane + peer)
            pick_copy(h, slot, k).start()
        picked[h, slot, plane - 1] = block_for(dom)

    def pick_copy(h, slot, k):
        return remote(
            chosen.at[h, slot, k], picked.at[h, slot, k], pick_sems, (h, slot, k),
            device(z, plane_peers[k], rep),
        )

    for h in range(halves):
        for above in range(2):
            @pl.when(passes_on(above))
            def _():
                line_copy(h, above, 0).start()
    for h in range(halves):
        choose(h, home, z, [x[b, :, half(h)] for b in range(own)])

    group_first = dom * group
    own_first = (dom * reps + rep) * own

    def each(count, body):
        if plan.ahead:
            for i in range(count):
                body(i)
        else:
            lax.fori_loop(0, count, lambda i, c: (body(i), c)[1], 0)

    def span(i):
        return pl.ds(pl.multiple_of(i * TILE, TILE), TILE)

    def build_wide(source, slot):
        def tile(other):
            s = source * plane + lax.rem(p + 2 * plane - 1 - other, plane)
            row, column = tile_row[dom, rep, s], tile_col[dom, rep, s]
            present = row >= 0
            limit = jnp.where(present, tile_count[dom, rep, s], 0)
            row_block = jnp.where(present, row, 0)
            left = across(left_ids[pl.ds(row_block, 1), :])
            right = right_ids[pl.ds(jnp.where(present, column, 0), 1), :]
            bits = bucket(left * (right + 1.0) + 3.0 * right)

            def place(b):
                here = jnp.where(row_block - group_first == b, limit, 0).astype(F32)
                wide[slot, span(b), span(other)] = jnp.where(bits < here, 1.0, 0.0).astype(BF16)

            each(group, place)

        each(plane, tile)

    def build_tall(target):
        s = target * plane + p
        first_own = (s * reps + rep) * own

        def tile(other):
            d = z * plane + lax.rem(p + 2 * plane - 1 - other, plane)
            row, column = tile_row[d, rep, s], tile_col[d, rep, s]
            present = row >= 0
            limit = jnp.where(present, tile_count[d, rep, s], 0)
            left = left_ids[pl.ds(jnp.where(present, row, 0), 1), :]
            right = across(right_ids[pl.ds(jnp.where(present, column, 0), 1), :])
            bits = bucket(left * (right + 1.0) + 3.0 * right)
            for b in range(own):
                here = jnp.where(column - first_own == b, limit, 0).astype(F32)
                tall[target, span(b), span(other)] = jnp.where(bits < here, 1.0, 0.0).astype(BF16)

        each(plane, tile)

    if plan.ahead:
        lax.fori_loop(0, line, lambda i, c: (build_wide(i, i), c)[1], 0)
    lax.fori_loop(0, line, lambda i, c: (build_tall(i), c)[1], 0)

    def count_degrees(s, carry):
        for other in range(reps):
            row, limit = tile_row[dom, other, s], tile_count[dom, other, s]
            carry = tuple(
                value + jnp.where(row == own_first + b, limit, 0) for b, value in enumerate(carry)
            )
        return carry

    degrees = lax.fori_loop(0, plan.doms, count_degrees, (jnp.int32(0),) * own)
    inverse = [
        1.0 / jnp.maximum(jnp.full((8, LANES), degree, jnp.int32).astype(F32), 1.0)[:1]
        for degree in degrees
    ]

    flat_x = x[...].reshape(own * TILE, plan.width_in)
    preact[...] = jnp.dot(flat_x, w_self[...], preferred_element_type=F32)

    def consume(h, slot, source, start):
        for k in range(plane - 1):
            pick_copy(h, slot, k).wait_recv()
        features = picked[h, slot].reshape(plane * TILE, LANES)
        if plan.ahead:
            value = jnp.dot(wide[source], features, preferred_element_type=F32)
            total[h] = value if start else total[h] + value
            return
        build_wide(source, 0)

        def rows(b):
            value = jnp.dot(wide[0, span(b)], features, preferred_element_type=F32)
            total[h, span(b)] = value if start else total[h, span(b)] + value

        each(group, rows)

    def arrive(h, above, k):
        line_copy(h, above, k - 1).wait_recv()

        if k < line - 1:
            @pl.when(passes_on(above))
            def _():
                line_copy(h, above, k).start()

        slot = slot_of(above, k)
        choose(h, slot, spot(above, k), [held[h, slot, b] for b in range(own)])

    def rep_copy(h, peer, slot):
        return remote(
            partial.at[h, peer], landed.at[h, slot], rep_sems, (h, slot), device(z, p, peer)
        )

    def send_partials(h):
        partial[h] = total[h].astype(BF16).reshape(reps, own, TILE, LANES)
        for k, peer in enumerate(rep_peers):
            rep_copy(h, peer, k).start()

    def consume_level(h, k):
        if k == 0:
            consume(h, home, z, True)
            return
        for above, k in levels[k - 1]:
            @pl.when(exists(above, k))
            def _():
                consume(h, slot_of(above, k), spot(above, k), False)

    for k in range(1, line):
        for h in range(halves):
            for above in range(2):
                @pl.when(exists(above, k))
                def _():
                    arrive(h, above, k)
        for h in range(halves):
            consume_level(h, k - 1)
    for h in range(halves):
        consume_level(h, line - 1)
        send_partials(h)

    for h in range(halves):
        for k, peer in enumerate(rep_peers):
            rep_copy(h, peer, k).wait_recv()
        for b in range(own):
            summed = partial[h, rep, b].astype(F32)
            for k in range(reps - 1):
                summed = summed + landed[h, k, b].astype(F32)
            mean[b * TILE : (b + 1) * TILE, half(h)] = (summed * inverse[b]).astype(BF16)
        preact[...] += jnp.dot(
            mean[:, half(h)], w_neigh[half(h), :], preferred_element_type=F32
        )
    value = preact[...]
    logistic = jax.nn.sigmoid(value)
    grad = (cot[...].astype(F32) * logistic * (1.0 + value * (1.0 - logistic))).astype(BF16)
    hidden[...] = (value * logistic).astype(BF16)

    def spread_copy(h, peer, slot):
        return remote(
            spread[h].at[rep], spread[h].at[rep], spread_sems, (h, slot), device(z, p, peer)
        )

    def spread_arrived(h, k):
        source = lax.rem(rep + reps - k - 1, reps)
        return remote(
            spread[h].at[source], spread[h].at[source], spread_sems, (h, k), device(z, p, source)
        )

    for h in range(halves):
        product = lax.dot_general(grad, w_neigh[half(h), :], OVER_COLS, preferred_element_type=F32)
        for b in range(own):
            spread[h][rep, b] = (product[b * TILE : (b + 1) * TILE] * inverse[b]).astype(BF16)
        for k, peer in enumerate(rep_peers):
            spread_copy(h, peer, k).start()

    both = (x[...].reshape(own * TILE, plan.width_in), mean[...])
    ring_at = col * reps + rep
    ring_peers = []
    for k in range(1, plan.ring):
        other = lax.rem(ring_at + k, plan.ring)
        ring_peers.append(
            (other, device(z, (other // reps) * plan.cores + core, lax.rem(other, reps)))
        )
    core_peers = []
    for k in range(1, plan.cores):
        other = lax.rem(core + k, plan.cores)
        core_peers.append((other, device(z, col * plan.cores + other, rep)))
    far_peers = [(other, device(other, p, rep)) for other in line_peers]

    stages = []
    if plan.split:
        for i, rows in enumerate(both):
            product = lax.dot_general(rows, grad, OVER_ROWS, preferred_element_type=F32)
            piece = product.astype(BF16).reshape(-1, plan.strip, plan.width_out)
            count = piece.shape[0]
            terms[i * count : (i + 1) * count] = piece
        per_core = plan.ring * plan.line

        def core_copies():
            return [
                remote(
                    terms.at[pl.ds(other * per_core, per_core)], first_in.at[k], core_sems, (k,), to
                )
                for k, (other, to) in enumerate(core_peers)
            ]

        def ring_copies():
            return [
                remote(
                    first.at[pl.ds(other * line, line)], second_in.at[k], ring_sems, (k,), to
                )
                for k, (other, to) in enumerate(ring_peers)
            ]

        def far_copies():
            return [
                remote(second.at[other], third_in.at[k], far_sems, (k,), to)
                for k, (other, to) in enumerate(far_peers)
            ]

        def place(c, q, zz):
            return (c * plan.ring + q) * line + zz

        def far_back_copies():
            return [
                remote(final, grads.at[place(core, ring_at, z)], far_back_sems, (k,), to)
                for k, (_, to) in enumerate(far_peers)
            ]

        def ring_back_copies():
            block = grads.at[pl.ds(place(core, ring_at, 0), line)]
            return [
                remote(block, block, ring_back_sems, (k,), to)
                for k, (_, to) in enumerate(ring_peers)
            ]

        def core_back_copies():
            block = grads.at[pl.ds(place(core, 0, 0), per_core)]
            return [
                remote(block, block, core_back_sems, (k,), to)
                for k, (_, to) in enumerate(core_peers)
            ]

        def start(copies):
            for copy in copies:
                copy.start()

        def arrived(copies):
            for copy in copies:
                copy.wait_recv()

        def stage_core():
            arrived(core_copies())
            value = terms[pl.ds(core * per_core, per_core)].astype(F32)
            for k in range(len(core_peers)):
                value = value + first_in[k].astype(F32)
            first[...] = value.astype(BF16)
            start(ring_copies())

        def stage_ring():
            arrived(ring_copies())
            value = first[pl.ds(ring_at * line, line)].astype(F32)
            for k in range(len(ring_peers)):
                value = value + second_in[k].astype(F32)
            second[...] = value.astype(BF16)
            start(far_copies())

        def stage_far():
            arrived(far_copies())
            value = second[z].astype(F32)
            for k in range(len(far_peers)):
                value = value + third_in[k].astype(F32)
            value = (value * scale).astype(BF16)
            final[...] = value
            grads[place(core, ring_at, z)] = value
            start(far_back_copies())

        def stage_ring_back():
            arrived(far_back_copies())
            start(ring_back_copies())

        def stage_core_back():
            arrived(ring_back_copies())
            start(core_back_copies())

        start(core_copies())
        stages = [stage_core, stage_ring, stage_far, stage_ring_back, stage_core_back]
    else:
        for i, rows in enumerate(both):
            grads[i] = lax.dot_general(rows, grad, OVER_ROWS, preferred_element_type=F32)

    def next_stage():
        if stages:
            stages.pop(0)()

    back[...] = lax.dot_general(grad, w_self[...], OVER_COLS, preferred_element_type=F32)

    def pick_back_copy(h, slot, k):
        return remote(
            chosen_back.at[h, slot, k], picked_back.at[h, slot, k], pick_back_sems, (h, slot, k),
            device(z, plane_peers[k], rep),
        )

    def choose_back(h, slot, target):
        def block_for(peer):
            row = tile_row[dom, rep, target * plane + peer]
            offset = jnp.minimum(jnp.maximum(row - group_first, 0), group - 1)
            return spread[h][offset // own, lax.rem(offset, own)]

        for k, peer in enumerate(plane_peers):
            chosen_back[h, slot, k] = block_for(peer)
            pick_back_copy(h, slot, k).start()
        picked_back[h, slot, plane - 1] = block_for(p)

    for h in range(halves):
        for k in range(reps - 1):
            spread_arrived(h, k).wait_recv()
        for level in reversed(levels):
            for above, k in level:
                @pl.when(exists(above, k))
                def _():
                    choose_back(h, slot_of(above, k), spot(above, k))
        choose_back(h, home, z)
    next_stage()

    def sum_copy(h, above, k):
        slot = slot_of(above, k)
        nearer = slot_of(above, k - 1) if k > 1 else home
        return remote(
            sums_out.at[h, slot], sums_in.at[above, h, nearer], sum_sems, (above, h, k - 1),
            device(z + 2 * above - 1, p, rep),
        )

    def contribution(h, slot, target):
        for k in range(plane - 1):
            pick_back_copy(h, slot, k).wait_recv()
        return jnp.dot(
            tall[target],
            picked_back[h, slot].reshape(plane * TILE, LANES),
            preferred_element_type=F32,
        )

    def pass_sums(h, above, k):
        slot = slot_of(above, k)
        value = contribution(h, slot, spot(above, k))
        sums_out[h, slot] = value.astype(BF16)
        if k < line - 1:
            @pl.when(passes_on(above))
            def _():
                sum_copy(h, above, k + 1).wait_recv()
                sums_out[h, slot] = (
                    sums_out[h, slot].astype(F32) + sums_in[above, h, slot].astype(F32)
                ).astype(BF16)

        sum_copy(h, above, k).start()

    for level in reversed(levels):
        for above, k in level:
            @pl.when(exists(above, k))
            def _():
                for h in range(halves):
                    pass_sums(h, above, k)
        next_stage()
    for h in range(halves):
        back[:, half(h)] += contribution(h, home, z)
        for above in range(2 if line > 1 else 0):
            @pl.when(passes_on(above))
            def _():
                sum_copy(h, above, 1).wait_recv()
                back[:, half(h)] += sums_in[above, h, home].astype(F32)
        feat_grad[:, half(h)] = back[:, half(h)].astype(BF16)
    while stages:
        next_stage()
    if plan.split:
        arrived(core_back_copies())

    for h in range(halves):
        for above in range(2):
            @pl.when(passes_on(above))
            def _():
                line_copy(h, above, 0).wait_send()
            for k in range(1, line):
                if k < line - 1:
                    @pl.when(jnp.logical_and(exists(above, k), passes_on(above)))
                    def _():
                        line_copy(h, above, k).wait_send()

                @pl.when(exists(above, k))
                def _():
                    sum_copy(h, above, k).wait_send()
        for slot in range(line):
            for k in range(plane - 1):
                pick_copy(h, slot, k).wait_send()
                pick_back_copy(h, slot, k).wait_send()
        for k, peer in enumerate(rep_peers):
            rep_copy(h, peer, k).wait_send()
            spread_copy(h, peer, k).wait_send()
    if plan.split:
        for copies in (
            core_copies(), ring_copies(), far_copies(),
            far_back_copies(), ring_back_copies(), core_back_copies(),
        ):
            for copy in copies:
                copy.wait_send()


def dma(*shape):
    return pltpu.SemaphoreType.DMA(tuple(max(size, 1) for size in (2,) + shape))


def shards(
    node_feats, node_ids, tile_row, tile_col, tile_count, self_weight, neigh_weight, out_grad
):
    rows, width_in = node_feats.shape
    width_out = self_weight.shape[1]
    plan = Plan(lax.axis_size("dom"), lax.axis_size("rep"), rows, width_in, width_out)
    line, plane, reps, own, halves = plan.line, plan.plane, plan.reps, plan.own, plan.halves
    scale = 1.0 / math.sqrt(rows * plan.doms * reps)
    id_rows = node_ids.shape[0] // TILE

    def buffer(*shape, dtype=BF16):
        return pltpu.VMEM(tuple(max(size, 1) for size in shape), dtype)

    tile = (TILE, LANES)
    scratch = [
        buffer(id_rows, TILE, dtype=F32),
        buffer(id_rows, TILE, dtype=F32),
        buffer(line if plan.ahead else 1, plan.group * TILE, plane * TILE),
        buffer(line, own * TILE, plane * TILE),
        buffer(halves, line, own, *tile),
        buffer(halves, line, plane, *tile),
        buffer(halves, line, plane, *tile),
        buffer(halves, plan.group * TILE, LANES, dtype=F32),
        buffer(halves, reps, own, *tile),
        buffer(halves, reps - 1, own, *tile),
        buffer(rows, width_in),
        buffer(rows, width_out, dtype=F32),
        buffer(rows, width_in, dtype=F32),
        *[buffer(reps, own, *tile) for _ in range(halves)],
        buffer(halves, line, plane, *tile),
        buffer(halves, line, plane, *tile),
        buffer(halves, line, own * TILE, LANES),
        buffer(2, halves, line, own * TILE, LANES),
    ]
    strip = (plan.strip, width_out)
    per_core = plan.ring * line
    if plan.split:
        scratch += [
            buffer(plan.cores * per_core, *strip),
            buffer(plan.cores - 1, per_core, *strip),
            buffer(per_core, *strip),
            buffer(plan.ring - 1, line, *strip),
            buffer(line, *strip),
            buffer(line - 1, *strip),
            buffer(*strip),
        ]
    scratch += [
        dma(2, halves, line),
        dma(halves, line, plane),
        dma(halves, reps - 1),
        dma(halves, reps - 1),
        dma(halves, line, plane),
        dma(2, halves, line),
    ]
    if plan.split:
        scratch += [
            dma(plan.cores - 1), dma(plan.ring - 1), dma(line - 1),
            dma(line - 1), dma(plan.ring - 1), dma(plan.cores - 1),
        ]
        grads_shape = jax.ShapeDtypeStruct((plan.cores * per_core, *strip), BF16)
    else:
        grads_shape = jax.ShapeDtypeStruct((2, width_in, width_out), F32)
    vmem, smem = pl.BlockSpec(memory_space=pltpu.VMEM), pl.BlockSpec(memory_space=pltpu.SMEM)
    hidden_out, feat_grad, grads = pl.pallas_call(
        functools.partial(fused, plan, scale),
        out_shape=(
            jax.ShapeDtypeStruct((rows, width_out), BF16),
            jax.ShapeDtypeStruct((rows, width_in), BF16),
            grads_shape,
        ),
        in_specs=[smem] * 3 + [vmem] * 5,
        out_specs=(vmem,) * 3,
        scratch_shapes=scratch,
        compiler_params=pltpu.CompilerParams(collective_id=1, has_side_effects=True),
    )(
        tile_row,
        tile_col,
        tile_count,
        node_ids.reshape(id_rows, TILE),
        node_feats.reshape(own, TILE, width_in),
        out_grad,
        self_weight,
        neigh_weight,
    )
    if plan.split:
        grads = grads.reshape(2, width_in, width_out).astype(F32)
    else:
        grads = lax.psum(grads, ("dom", "rep")) * scale
    return hidden_out, feat_grad, grads[0], grads[1]


def solution(mesh):
    placed = (P(("dom", "rep"), None), P(), P(), P(), P(), P(), P(), P(("dom", "rep"), None))
    return jax.shard_map(
        shards,
        mesh=mesh,
        in_specs=placed,
        out_specs=(P(("dom", "rep"), None), P(("dom", "rep"), None), P(), P()),
        check_vma=False,
    )
```

time: 111 us -> 70.9 us (0.64)
  waiting for transfers between devices: 19 us -> 0 us
  starting transfers between devices: 13.7 us -> 0 us
  Pallas kernels: 53.9 us -> 66.1 us
  local copies, waits for them, and re-layouts: 11 us -> 3.92 us
  matrix products: 6.44 us -> 0 us
  other arithmetic: 4.96 us -> 0 us
    all_to_all x2 -> x0, waiting for transfers between devices: 19 us -> none  [the longest x1 19 us: shards(): lax.all_to_all(outgoing, 'dom', split_axis=0, concat_axis=0, tiled=True)]
    all_to_all x2 -> x0, starting transfers between devices: 13.7 us -> none  [the longest x1 7.39 us: shards(): lax.all_to_all(outgoing, 'dom', split_axis=0, concat_axis=0, tiled=True)]
    pallas_call x2 -> x1, Pallas kernels: 53.9 us -> 66.1 us  [shards(): pl.pallas_call(functools.partial(fused, plan, scale), out_shape=(jax.Shap...]
    dot_general x4 -> x0, matrix products: 6.44 us -> none  [the longest x1 2.87 us: shards(): jnp.einsum('sij,sif->sjf', inbound_masks, picked_rows, preferred_element_...]
    gather x4 -> x0, local copies, waits for them, and re-layouts: 5.24 us -> none  [the longest x1 2.51 us: shards(): outgoing = feat_blocks[outbound_offset]]
    select_n x6 -> x0, other arithmetic: 2.11 us -> none  [the longest x1 0.7 us: shards(): id_blocks[inbound_block]]
    sub x1 -> x0, other arithmetic: 1.45 us -> none  [shards(): outbound_offset = jnp.where(outbound_present, outbound_cols - own_first, 0)]
  transfers between devices with their start and end apart: 2 -> 0, of which waited for: 1 -> 0; matrix products, arithmetic and copies ran while one was open for 6% -> 0% of each run, Pallas kernels for 33% -> 0%
where the time goes in v1:
time: 70.9 us; the launch traced here: 70.7 us
  Pallas kernels  66.1 us (93%)
  local copies, waits for them, and re-layouts  3.92 us (6%)
    pallas_call x1, Pallas kernels, shards(): pl.pallas_call(functools.partial(fused, plan, scale), out_shape=(jax.Shap...  66.1 us
    slice x1, local copies, waits for them, and re-layouts, shards(): return (hidden_out, feat_grad, grads[0], grads[1])  2.18 us
    unnamed x6, local copies, waits for them, and re-layouts  1.75 us

profile of v1, /device:TPU:0, one launch (start us, length us, event | category | flops | bytes accessed | tf_op | source)
XLA Modules:
  0.0 70.7 jit_solution(9421071668024970217)
XLA Ops:
  0.6 66.1 %shard_map.111 = (bf16[384,512]{1,0:T(8,128)(2,1)}, bf16[384,256]{1,0:T(8,128)(2,1)}, bf16[32,16,512]{2,1,0:T(8,128)(2,1)}) custom-call(s32[16,2,16]{2,1,0:T(2,128)} %refs_0_.1, s32[16,2,16]{2,1,0:T(2,128)} %refs_1_.1, s32[16,2,16]{2,1,0:T(2,128)} %refs_2_.1, s32[96,128]{1,0:T(8,128)} %bitcast.7, bf16[3,128,256]{2,1,0:T(8,128)(2,1)} %bitcast.6, ...), custom_call_target="tpu_custom_call" | custom-call | tf_op jit(solution)/shard_map/pallas_call | solution.py:628
  66.8 0.0 copy-start
  66.8 2.2 %fusion = (f32[16,16,512]{2,1,0:T(8,128)}, f32[16,16,512]{2,1,0:T(8,128)}) fusion(bf16[32,16,512]{2,1,0:T(8,128)(2,1)} %get-tuple-element.9), kind=kLoop, calls=%fused_computation | loop fusion | bytes 2097152 | tf_op jit(solution)/shard_map/slice | solution.py:653
  68.9 0.0 copy-done
  68.9 0.0 copy-start.1
  68.9 0.7 %copy.14 = bf16[384,512]{1,0:T(8,128)(2,1)} copy(bf16[384,512]{1,0:T(8,128)(2,1)S(1)} %copy-done) | data formatting | bytes 786432
  69.7 0.3 copy-done.1
  70.0 0.7 copy.15
Async XLA Ops:
  66.8 2.2 %copy-start = (bf16[384,512]{1,0:T(8,128)(2,1)S(1)}, bf16[384,512]{1,0:T(8,128)(2,1)}, u32[]{:S(2)}) copy-start(bf16[384,512]{1,0:T(8,128)(2,1)} %get-tuple-element.16) | copy-start | bytes 1179652
  68.9 1.1 %copy-start.1 = (bf16[384,256]{1,0:T(8,128)(2,1)S(1)}, bf16[384,256]{1,0:T(8,128)(2,1)}, u32[]{:S(2)}) copy-start(bf16[384,256]{1,0:T(8,128)(2,1)} %get-tuple-element.17) | copy-start | bytes 589828

commit v2 on v1

--- a/solution.py
+++ b/solution.py
@@ -48,7 +48,7 @@
         self.width_in, self.width_out = width_in, width_out
         self.ring = self.cols * rep_total
         self.strip = 2 * width_in // (self.cores * self.ring * self.line)
-        self.split = self.strip % 16 == 0
+        self.split = self.strip % 16 == 0 and self.cores == 2
         self.ahead = self.line * self.group * self.plane * TILE * TILE * 2 <= 2**23
 
 
@@ -62,17 +62,20 @@
     line, plane, reps, own, group, halves = (
         plan.line, plan.plane, plan.reps, plan.own, plan.group, plan.halves,
     )
-    tile_row, tile_col, tile_count, ids, x, cot, w_self, w_neigh = take(8)
+    given = take(8)
     hidden, feat_grad, grads = take(3)
+    inputs = take(8)
+    tile_row, tile_col, tile_count, ids, x, cot, w_self, w_neigh = inputs
     left_ids, right_ids, wide, tall = take(4)
     held, chosen, picked, total, partial, landed, mean, preact, back = take(9)
     spread = take(halves)
     picked_back, chosen_back, sums_out, sums_in = take(4)
     if plan.split:
         terms, first_in, first, second_in, second, third_in, final = take(7)
+    (load_sems,) = take(1)
     line_sems, pick_sems, rep_sems, spread_sems, pick_back_sems, sum_sems = take(6)
     if plan.split:
-        core_sems, ring_sems, far_sems, far_back_sems, ring_back_sems, core_back_sems = take(6)
+        core_sems, far_sems, ring_sems, far_back_sems, ring_back_sems, core_back_sems = take(6)
 
     dom, rep = lax.axis_index("dom"), lax.axis_index("rep")
     z, p = dom // plane, lax.rem(dom, plane)
@@ -100,10 +103,18 @@
     for k in range(plan.cols):
         other = lax.rem(col + k, plan.cols) * plan.cores + core
         everyone += [device(z, other, peer) for peer in rep_peers]
+    loads = [
+        pltpu.make_async_copy(src, dst, load_sems.at[i])
+        for i, (src, dst) in enumerate(zip(given, inputs))
+    ]
+    for i in (4, 1, 3, 0, 2, 6, 7, 5):
+        loads[i].start()
     barrier = pltpu.get_barrier_semaphore()
     for peer in everyone:
         pl.semaphore_signal(barrier, inc=1, device_id=peer, device_id_type=MESH)
 
+    for i in (0, 1, 2, 3, 4):
+        loads[i].wait()
     node = ids[...].astype(F32)
     left_ids[...] = modulo(node, 4093.0)
     right_ids[...] = modulo(node, 4091.0)
@@ -232,6 +243,8 @@
         for degree in degrees
     ]
 
+    for i in (5, 6, 7):
+        loads[i].wait()
     flat_x = x[...].reshape(own * TILE, plan.width_in)
     preact[...] = jnp.dot(flat_x, w_self[...], preferred_element_type=F32)
 
@@ -307,7 +320,6 @@
     value = preact[...]
     logistic = jax.nn.sigmoid(value)
     grad = (cot[...].astype(F32) * logistic * (1.0 + value * (1.0 - logistic))).astype(BF16)
-    hidden[...] = (value * logistic).astype(BF16)
 
     def spread_copy(h, peer, slot):
         return remote(
@@ -345,51 +357,41 @@
     if plan.split:
         for i, rows in enumerate(both):
             product = lax.dot_general(rows, grad, OVER_ROWS, preferred_element_type=F32)
-            piece = product.astype(BF16).reshape(-1, plan.strip, plan.width_out)
-            count = piece.shape[0]
-            terms[i * count : (i + 1) * count] = piece
-        per_core = plan.ring * plan.line
+            terms[i] = product.astype(BF16).reshape(line, plan.ring, plan.strip, plan.width_out)
 
         def core_copies():
             return [
-                remote(
-                    terms.at[pl.ds(other * per_core, per_core)], first_in.at[k], core_sems, (k,), to
-                )
+                remote(terms.at[other], first_in.at[k], core_sems, (k,), to)
                 for k, (other, to) in enumerate(core_peers)
             ]
 
+        def far_copies():
+            return [
+                remote(first.at[other], second_in.at[k], far_sems, (k,), to)
+                for k, (other, to) in enumerate(far_peers)
+            ]
+
         def ring_copies():
             return [
-                remote(
-                    first.at[pl.ds(other * line, line)], second_in.at[k], ring_sems, (k,), to
-                )
+                remote(second.at[other], third_in.at[k], ring_sems, (k,), to)
                 for k, (other, to) in enumerate(ring_peers)
             ]
 
-        def far_copies():
-            return [
-                remote(second.at[other], third_in.at[k], far_sems, (k,), to)
-                for k, (other, to) in enumerate(far_peers)
-            ]
-
-        def place(c, q, zz):
-            return (c * plan.ring + q) * line + zz
-
         def far_back_copies():
             return [
-                remote(final, grads.at[place(core, ring_at, z)], far_back_sems, (k,), to)
+                remote(final, grads.at[core, z, ring_at], far_back_sems, (k,), to)
                 for k, (_, to) in enumerate(far_peers)
             ]
 
         def ring_back_copies():
-            block = grads.at[pl.ds(place(core, ring_at, 0), line)]
+            block = grads.at[core, :, ring_at]
             return [
                 remote(block, block, ring_back_sems, (k,), to)
                 for k, (_, to) in enumerate(ring_peers)
             ]
 
         def core_back_copies():
-            block = grads.at[pl.ds(place(core, 0, 0), per_core)]
+            block = grads.at[core]
             return [
                 remote(block, block, core_back_sems, (k,), to)
                 for k, (_, to) in enumerate(core_peers)
@@ -405,28 +407,28 @@
 
         def stage_core():
             arrived(core_copies())
-            value = terms[pl.ds(core * per_core, per_core)].astype(F32)
+            value = terms[core].astype(F32)
             for k in range(len(core_peers)):
                 value = value + first_in[k].astype(F32)
             first[...] = value.astype(BF16)
+            start(far_copies())
+
+        def stage_far():
+            arrived(far_copies())
+            value = first[z].astype(F32)
+            for k in range(len(far_peers)):
+                value = value + second_in[k].astype(F32)
+            second[...] = value.astype(BF16)
             start(ring_copies())
 
         def stage_ring():
             arrived(ring_copies())
-            value = first[pl.ds(ring_at * line, line)].astype(F32)
+            value = second[ring_at].astype(F32)
             for k in range(len(ring_peers)):
-                value = value + second_in[k].astype(F32)
-            second[...] = value.astype(BF16)
-            start(far_copies())
-
-        def stage_far():
-            arrived(far_copies())
-            value = second[z].astype(F32)
-            for k in range(len(far_peers)):
                 value = value + third_in[k].astype(F32)
             value = (value * scale).astype(BF16)
             final[...] = value
-            grads[place(core, ring_at, z)] = value
+            grads[core, z, ring_at] = value
             start(far_back_copies())
 
         def stage_ring_back():
@@ -438,7 +440,7 @@
             start(core_back_copies())
 
         start(core_copies())
-        stages = [stage_core, stage_ring, stage_far, stage_ring_back, stage_core_back]
+        stages = [stage_core, stage_far, stage_ring, stage_ring_back, stage_core_back]
     else:
         for i, rows in enumerate(both):
             grads[i] = lax.dot_general(rows, grad, OVER_ROWS, preferred_element_type=F32)
@@ -447,7 +449,9 @@
         if stages:
             stages.pop(0)()
 
+    hidden[...] = (value * logistic).astype(BF16)
     back[...] = lax.dot_general(grad, w_self[...], OVER_COLS, preferred_element_type=F32)
+    next_stage()
 
     def pick_back_copy(h, slot, k):
         return remote(
@@ -466,16 +470,20 @@
             pick_back_copy(h, slot, k).start()
         picked_back[h, slot, plane - 1] = block_for(p)
 
-    for h in range(halves):
-        for k in range(reps - 1):
-            spread_arrived(h, k).wait_recv()
-        for level in reversed(levels):
-            for above, k in level:
-                @pl.when(exists(above, k))
+    order = [place for level in reversed(levels) for place in level] + [None]
+    for i, place_at in enumerate(order):
+        for h in range(halves):
+            if i == 0:
+                for k in range(reps - 1):
+                    spread_arrived(h, k).wait_recv()
+            if place_at is None:
+                choose_back(h, home, z)
+            else:
+                @pl.when(exists(*place_at))
                 def _():
-                    choose_back(h, slot_of(above, k), spot(above, k))
-        choose_back(h, home, z)
-    next_stage()
+                    choose_back(h, slot_of(*place_at), spot(*place_at))
+        if i + 1 == len(order) - 1 - 2 * (line > 1):
+            next_stage()
 
     def sum_copy(h, above, k):
         slot = slot_of(above, k)
@@ -514,8 +522,12 @@
             def _():
                 for h in range(halves):
                     pass_sums(h, above, k)
-        next_stage()
+        if level is levels[min(1, line - 2)]:
+            next_stage()
+    next_stage()
     for h in range(halves):
+        if h == 1:
+            next_stage()
         back[:, half(h)] += contribution(h, home, z)
         for above in range(2 if line > 1 else 0):
             @pl.when(passes_on(above))
@@ -558,6 +570,23 @@
                 copy.wait_send()
 
 
+def write_out(hidden, feat_grad, grads, *refs):
+    outs, (wide_grads, sems) = refs[:4], refs[4:]
+    copies = [
+        pltpu.make_async_copy(src, dst, sems.at[i])
+        for i, (src, dst) in enumerate(
+            zip((hidden, feat_grad, wide_grads.at[0], wide_grads.at[1]), outs)
+        )
+    ]
+    copies[0].start()
+    copies[1].start()
+    for i in range(2):
+        wide_grads[i] = grads[i].astype(F32).reshape(wide_grads.shape[1:])
+        copies[2 + i].start()
+    for copy in copies:
+        copy.wait()
+
+
 def dma(*shape):
     return pltpu.SemaphoreType.DMA(tuple(max(size, 1) for size in (2,) + shape))
 
@@ -576,7 +605,16 @@
         return pltpu.VMEM(tuple(max(size, 1) for size in shape), dtype)
 
     tile = (TILE, LANES)
+    tables = pltpu.SMEM(tile_row.shape, jnp.int32)
     scratch = [
+        tables,
+        tables,
+        tables,
+        buffer(id_rows, TILE, dtype=jnp.int32),
+        buffer(own, TILE, width_in),
+        buffer(rows, width_out),
+        buffer(width_in, width_out),
+        buffer(width_in, width_out),
         buffer(id_rows, TILE, dtype=F32),
         buffer(id_rows, TILE, dtype=F32),
         buffer(line if plan.ahead else 1, plan.group * TILE, plane * TILE),
@@ -597,18 +635,18 @@
         buffer(2, halves, line, own * TILE, LANES),
     ]
     strip = (plan.strip, width_out)
-    per_core = plan.ring * line
     if plan.split:
         scratch += [
-            buffer(plan.cores * per_core, *strip),
-            buffer(plan.cores - 1, per_core, *strip),
-            buffer(per_core, *strip),
-            buffer(plan.ring - 1, line, *strip),
-            buffer(line, *strip),
-            buffer(line - 1, *strip),
+            buffer(plan.cores, line, plan.ring, *strip),
+            buffer(plan.cores - 1, line, plan.ring, *strip),
+            buffer(line, plan.ring, *strip),
+            buffer(line - 1, plan.ring, *strip),
+            buffer(plan.ring, *strip),
+            buffer(plan.ring - 1, *strip),
             buffer(*strip),
         ]
     scratch += [
+        pltpu.SemaphoreType.DMA((8,)),
         dma(2, halves, line),
         dma(halves, line, plane),
         dma(halves, reps - 1),
@@ -618,21 +656,21 @@
     ]
     if plan.split:
         scratch += [
-            dma(plan.cores - 1), dma(plan.ring - 1), dma(line - 1),
+            dma(plan.cores - 1), dma(line - 1), dma(plan.ring - 1),
             dma(line - 1), dma(plan.ring - 1), dma(plan.cores - 1),
         ]
-        grads_shape = jax.ShapeDtypeStruct((plan.cores * per_core, *strip), BF16)
+        grads_shape = jax.ShapeDtypeStruct((plan.cores, line, plan.ring, *strip), BF16)
     else:
         grads_shape = jax.ShapeDtypeStruct((2, width_in, width_out), F32)
-    vmem, smem = pl.BlockSpec(memory_space=pltpu.VMEM), pl.BlockSpec(memory_space=pltpu.SMEM)
+    vmem, anywhere = pl.BlockSpec(memory_space=pltpu.VMEM), pl.BlockSpec(memory_space=pl.ANY)
     hidden_out, feat_grad, grads = pl.pallas_call(
         functools.partial(fused, plan, scale),
         out_shape=(
-            jax.ShapeDtypeStruct((rows, width_out), BF16),
-            jax.ShapeDtypeStruct((rows, width_in), BF16),
-            grads_shape,
+            pltpu.VMEM((rows, width_out), BF16),
+            pltpu.VMEM((rows, width_in), BF16),
+            pltpu.VMEM(grads_shape.shape, grads_shape.dtype),
         ),
-        in_specs=[smem] * 3 + [vmem] * 5,
+        in_specs=[anywhere] * 8,
         out_specs=(vmem,) * 3,
         scratch_shapes=scratch,
         compiler_params=pltpu.CompilerParams(collective_id=1, has_side_effects=True),
@@ -646,11 +684,26 @@
         self_weight,
         neigh_weight,
     )
-    if plan.split:
-        grads = grads.reshape(2, width_in, width_out).astype(F32)
-    else:
+    if not plan.split:
         grads = lax.psum(grads, ("dom", "rep")) * scale
-    return hidden_out, feat_grad, grads[0], grads[1]
+        return hidden_out, feat_grad, grads[0], grads[1]
+    grad_shape = jax.ShapeDtypeStruct((width_in, width_out), F32)
+    return pl.pallas_call(
+        write_out,
+        out_shape=(
+            jax.ShapeDtypeStruct((rows, width_out), BF16),
+            jax.ShapeDtypeStruct((rows, width_in), BF16),
+            grad_shape,
+            grad_shape,
+        ),
+        in_specs=[vmem] * 3,
+        out_specs=(anywhere,) * 4,
+        scratch_shapes=[
+            buffer(2, width_in, width_out, dtype=F32),
+            pltpu.SemaphoreType.DMA((4,)),
+        ],
+        compiler_params=pltpu.CompilerParams(vmem_limit_bytes=2**23),
+    )(hidden_out, feat_grad, grads)
 
 
 def solution(mesh):

time: 70.9 us -> 60.4 us (0.85)
  Pallas kernels: 66.1 us -> 59.6 us
  local copies, waits for them, and re-layouts: 3.92 us -> 0 us
    pallas_call x1 -> x2, Pallas kernels: 66.1 us -> 59.6 us  [the longest x1 58.4 us: shards(): pl.pallas_call(functools.partial(fused, plan, scale), out_shape=(pltpu.VM...]
    slice x1 -> x0, local copies, waits for them, and re-layouts: 2.18 us -> none  [shards(): return (hidden_out, feat_grad, grads[0], grads[1])]
    unnamed x6 -> x0, local copies, waits for them, and re-layouts: 1.75 us -> none
where the time goes in v2:
time: 60.4 us; the launch traced here: 60.2 us
  Pallas kernels  59.6 us (99%)
  between operations  0.64 us (1%)
    pallas_call x1, Pallas kernels, shards(): pl.pallas_call(functools.partial(fused, plan, scale), out_shape=(pltpu.VM...  58.4 us

profile of v2, /device:TPU:0, one launch (start us, length us, event | category | flops | bytes accessed | tf_op | source)
XLA Modules:
  0.0 60.2 jit_solution(2431479399318489509)
XLA Ops:
  0.6 58.4 %shard_map.111 = (bf16[384,512]{1,0:T(8,128)(2,1)S(1)}, bf16[384,256]{1,0:T(8,128)(2,1)S(1)}, bf16[2,4,4,16,512]{4,3,2,1,0:T(8,128)(2,1)S(1)}) custom-call(s32[16,2,16]{2,1,0:T(2,128)} %refs_0_.1, s32[16,2,16]{2,1,0:T(2,128)} %refs_1_.1, s32[16,2,16]{2,1,0:T(2,128)} %refs_2_.1, s32[96,128]{1,0:T(8,128)} %bitcast.3, bf16[3,128,256]{2,1,0:T(8,128)(2,1)} %bitcast.2, ...), custom_call_target="tpu_custom_call" | custom-call | tf_op jit(solution)/shard_map/pallas_call | solution.py:666
  59.0 1.2 %shard_map.112 = (bf16[384,512]{1,0:T(8,128)(2,1)}, bf16[384,256]{1,0:T(8,128)(2,1)}, f32[256,512]{1,0:T(8,128)}, f32[256,512]{1,0:T(8,128)}) custom-call(bf16[384,512]{1,0:T(8,128)(2,1)S(1)} %get-tuple-element.7.hidden, bf16[384,256]{1,0:T(8,128)(2,1)S(1)} %get-tuple-element.8.feat_grad, bf16[2,4,4,16,512]{4,3,2,1,0:T(8,128)(2,1)S(1)} %get-tuple-element.9.grads), custom_call_target="tpu_custom_call" | custom-call | tf_op jit(solution)/shard_map/pallas_call | solution.py:691

commit v3 on v2

--- a/solution.py
+++ b/solution.py
@@ -470,20 +470,20 @@
             pick_back_copy(h, slot, k).start()
         picked_back[h, slot, plane - 1] = block_for(p)
 
-    order = [place for level in reversed(levels) for place in level] + [None]
-    for i, place_at in enumerate(order):
-        for h in range(halves):
-            if i == 0:
-                for k in range(reps - 1):
-                    spread_arrived(h, k).wait_recv()
-            if place_at is None:
-                choose_back(h, home, z)
-            else:
-                @pl.when(exists(*place_at))
-                def _():
-                    choose_back(h, slot_of(*place_at), spot(*place_at))
-        if i + 1 == len(order) - 1 - 2 * (line > 1):
-            next_stage()
+    for h in range(halves):
+        for k in range(reps - 1):
+            spread_arrived(h, k).wait_recv()
+        for above, k in (levels[-1] if levels else []):
+            @pl.when(exists(above, k))
+            def _():
+                choose_back(h, slot_of(above, k), spot(above, k))
+
+    def choose_level(level):
+        for above, k in level:
+            @pl.when(exists(above, k))
+            def _():
+                for h in range(halves):
+                    choose_back(h, slot_of(above, k), spot(above, k))
 
     def sum_copy(h, above, k):
         slot = slot_of(above, k)
@@ -516,18 +516,39 @@
 
         sum_copy(h, above, k).start()
 
-    for level in reversed(levels):
-        for above, k in level:
-            @pl.when(exists(above, k))
+    upper = 2 * z >= line
+
+    def pass_level(level):
+        for above, k, turn in [(1, k, upper) for _, k in level[:1]] + [
+            (0, k, None) for _, k in level[:1]
+        ] + [(1, k, jnp.logical_not(upper)) for _, k in level[:1]]:
+            here = exists(above, k)
+
+            @pl.when(here if turn is None else jnp.logical_and(here, turn))
             def _():
                 for h in range(halves):
                     pass_sums(h, above, k)
-        if level is levels[min(1, line - 2)]:
-            next_stage()
+
+    turn = stages.pop(1) if len(stages) > 1 else None
+    for level in reversed(levels[-2:-1]):
+        choose_level(level)
+    for level in levels[-1:]:
+        pass_level(level)
     next_stage()
-    for h in range(halves):
-        if h == 1:
-            next_stage()
+    for level in reversed(levels[:-2]):
+        choose_level(level)
+    for h in range(halves):
+        choose_back(h, home, z)
+    rest = levels[:-1]
+    if turn:
+        turn()
+    for level in rest[-1:]:
+        pass_level(level)
+    next_stage()
+    for level in reversed(rest[:-1]):
+        pass_level(level)
+    next_stage()
+    for h in range(halves):
         back[:, half(h)] += contribution(h, home, z)
         for above in range(2 if line > 1 else 0):
             @pl.when(passes_on(above))

time: 60.4 us -> 56.4 us (0.934)
  Pallas kernels: 59.6 us -> 55.6 us
    pallas_call x1, Pallas kernels: 58.4 us -> 54.4 us  [shards(): pl.pallas_call(functools.partial(fused, plan, scale), out_shape=(pltpu.VM...]
where the time goes in v3:
time: 56.4 us; the launch traced here: 56.3 us
  Pallas kernels  55.6 us (99%)
  between operations  0.64 us (1%)
    pallas_call x1, Pallas kernels, shards(): pl.pallas_call(functools.partial(fused, plan, scale), out_shape=(pltpu.VM...  54.4 us
    pallas_call x1, Pallas kernels, shards(): pl.pallas_call(write_out, out_shape=(jax.ShapeDtypeStruct((rows, width_ou...  1.2 us

profile of v3, /device:TPU:0, one launch (start us, length us, event | category | flops | bytes accessed | tf_op | source)
XLA Modules:
  0.0 56.3 jit_solution(17961191884546403698)
XLA Ops:
  0.6 54.4 %shard_map.111 = (bf16[384,512]{1,0:T(8,128)(2,1)S(1)}, bf16[384,256]{1,0:T(8,128)(2,1)S(1)}, bf16[2,4,4,16,512]{4,3,2,1,0:T(8,128)(2,1)S(1)}) custom-call(s32[16,2,16]{2,1,0:T(2,128)} %refs_0_.1, s32[16,2,16]{2,1,0:T(2,128)} %refs_1_.1, s32[16,2,16]{2,1,0:T(2,128)} %refs_2_.1, s32[96,128]{1,0:T(8,128)} %bitcast.3, bf16[3,128,256]{2,1,0:T(8,128)(2,1)} %bitcast.2, ...), custom_call_target="tpu_custom_call" | custom-call | tf_op jit(solution)/shard_map/pallas_call | solution.py:687
  55.1 1.2 %shard_map.112 = (bf16[384,512]{1,0:T(8,128)(2,1)}, bf16[384,256]{1,0:T(8,128)(2,1)}, f32[256,512]{1,0:T(8,128)}, f32[256,512]{1,0:T(8,128)}) custom-call(bf16[384,512]{1,0:T(8,128)(2,1)S(1)} %get-tuple-element.7.hidden, bf16[384,256]{1,0:T(8,128)(2,1)S(1)} %get-tuple-element.8.feat_grad, bf16[2,4,4,16,512]{4,3,2,1,0:T(8,128)(2,1)S(1)} %get-tuple-element.9.grads), custom_call_target="tpu_custom_call" | custom-call | tf_op jit(solution)/shard_map/pallas_call | solution.py:712

commit v4 on v3

--- a/solution.py
+++ b/solution.py
@@ -113,11 +113,6 @@
     for peer in everyone:
         pl.semaphore_signal(barrier, inc=1, device_id=peer, device_id_type=MESH)
 
-    for i in (0, 1, 2, 3, 4):
-        loads[i].wait()
-    node = ids[...].astype(F32)
-    left_ids[...] = modulo(node, 4093.0)
-    right_ids[...] = modulo(node, 4091.0)
 
     home = line - 1
     levels = [[(above, k) for above in range(2)] for k in range(1, line)]
@@ -144,6 +139,7 @@
             src, held.at[h, slot], line_sems, (above, h, k), device(z + 1 - 2 * above, p, rep)
         )
 
+    loads[4].wait()
     pl.semaphore_wait(barrier, len(everyone))
 
     def choose(h, slot, source, blocks):
@@ -172,6 +168,11 @@
             @pl.when(passes_on(above))
             def _():
                 line_copy(h, above, 0).start()
+    for i in range(4):
+        loads[i].wait()
+    node = ids[...].astype(F32)
+    left_ids[...] = modulo(node, 4093.0)
+    right_ids[...] = modulo(node, 4091.0)
     for h in range(halves):
         choose(h, home, z, [x[b, :, half(h)] for b in range(own)])
 
@@ -519,14 +520,14 @@
     upper = 2 * z >= line
 
     def pass_level(level):
-        for above, k, turn in [(1, k, upper) for _, k in level[:1]] + [
-            (0, k, None) for _, k in level[:1]
-        ] + [(1, k, jnp.logical_not(upper)) for _, k in level[:1]]:
-            here = exists(above, k)
-
-            @pl.when(here if turn is None else jnp.logical_and(here, turn))
-            def _():
-                for h in range(halves):
+        for h in range(halves):
+            for above, k, turn in [(1, k, upper) for _, k in level[:1]] + [
+                (0, k, None) for _, k in level[:1]
+            ] + [(1, k, jnp.logical_not(upper)) for _, k in level[:1]]:
+                here = exists(above, k)
+
+                @pl.when(here if turn is None else jnp.logical_and(here, turn))
+                def _():
                     pass_sums(h, above, k)
 
     turn = stages.pop(1) if len(stages) > 1 else None
@@ -544,9 +545,18 @@
         turn()
     for level in rest[-1:]:
         pass_level(level)
-    next_stage()
+    at_end = z * (line - 1 - z) == 0
+    turn = stages.pop(0) if stages else None
+    if turn:
+        @pl.when(jnp.logical_not(at_end))
+        def _():
+            turn()
     for level in reversed(rest[:-1]):
         pass_level(level)
+    if turn:
+        @pl.when(at_end)
+        def _():
+            turn()
     next_stage()
     for h in range(halves):
         back[:, half(h)] += contribution(h, home, z)

time: 56.4 us -> 56.3 us (level)
  no operation moved by 1% of the time
where the time goes in v4:
time: 56.3 us; the launch traced here: 56.2 us
  Pallas kernels  55.5 us (99%)
  between operations  0.64 us (1%)
    pallas_call x1, Pallas kernels, shards(): pl.pallas_call(functools.partial(fused, plan, scale), out_shape=(pltpu.VM...  54.3 us
    pallas_call x1, Pallas kernels, shards(): pl.pallas_call(write_out, out_shape=(jax.ShapeDtypeStruct((rows, width_ou...  1.2 us

profile of v4, /device:TPU:0, one launch (start us, length us, event | category | flops | bytes accessed | tf_op | source)
XLA Modules:
  0.0 56.2 jit_solution(14979842895417130404)
XLA Ops:
  0.6 54.3 %shard_map.111 = (bf16[384,512]{1,0:T(8,128)(2,1)S(1)}, bf16[384,256]{1,0:T(8,128)(2,1)S(1)}, bf16[2,4,4,16,512]{4,3,2,1,0:T(8,128)(2,1)S(1)}) custom-call(s32[16,2,16]{2,1,0:T(2,128)} %refs_0_.1, s32[16,2,16]{2,1,0:T(2,128)} %refs_1_.1, s32[16,2,16]{2,1,0:T(2,128)} %refs_2_.1, s32[96,128]{1,0:T(8,128)} %bitcast.3, bf16[3,128,256]{2,1,0:T(8,128)(2,1)} %bitcast.2, ...), custom_call_target="tpu_custom_call" | custom-call | tf_op jit(solution)/shard_map/pallas_call | solution.py:697
  55.0 1.2 %shard_map.112 = (bf16[384,512]{1,0:T(8,128)(2,1)}, bf16[384,256]{1,0:T(8,128)(2,1)}, f32[256,512]{1,0:T(8,128)}, f32[256,512]{1,0:T(8,128)}) custom-call(bf16[384,512]{1,0:T(8,128)(2,1)S(1)} %get-tuple-element.7.hidden, bf16[384,256]{1,0:T(8,128)(2,1)S(1)} %get-tuple-element.8.feat_grad, bf16[2,4,4,16,512]{4,3,2,1,0:T(8,128)(2,1)S(1)} %get-tuple-element.9.grads), custom_call_target="tpu_custom_call" | custom-call | tf_op jit(solution)/shard_map/pallas_call | solution.py:722

commit v5 on v4

--- a/solution.py
+++ b/solution.py
@@ -333,13 +333,14 @@
             spread[h].at[source], spread[h].at[source], spread_sems, (h, k), device(z, p, source)
         )
 
-    for h in range(halves):
+    def spread_half(h):
         product = lax.dot_general(grad, w_neigh[half(h), :], OVER_COLS, preferred_element_type=F32)
         for b in range(own):
             spread[h][rep, b] = (product[b * TILE : (b + 1) * TILE] * inverse[b]).astype(BF16)
         for k, peer in enumerate(rep_peers):
             spread_copy(h, peer, k).start()
 
+    spread_half(0)
     both = (x[...].reshape(own * TILE, plan.width_in), mean[...])
     ring_at = col * reps + rep
     ring_peers = []
@@ -450,9 +451,11 @@
         if stages:
             stages.pop(0)()
 
+    for h in range(1, halves):
+        spread_half(h)
     hidden[...] = (value * logistic).astype(BF16)
+    next_stage()
     back[...] = lax.dot_general(grad, w_self[...], OVER_COLS, preferred_element_type=F32)
-    next_stage()
 
     def pick_back_copy(h, slot, k):
         return remote(

time: 56.3 us -> 56.3 us (level)
  no operation moved by 1% of the time
where the time goes in v5:
time: 56.3 us; the launch traced here: 56.2 us
  Pallas kernels  55.5 us (99%)
  between operations  0.64 us (1%)
    pallas_call x1, Pallas kernels, shards(): pl.pallas_call(functools.partial(fused, plan, scale), out_shape=(pltpu.VM...  54.3 us
    pallas_call x1, Pallas kernels, shards(): pl.pallas_call(write_out, out_shape=(jax.ShapeDtypeStruct((rows, width_ou...  1.2 us

profile of v5, /device:TPU:0, one launch (start us, length us, event | category | flops | bytes accessed | tf_op | source)
XLA Modules:
  0.0 56.2 jit_solution(2906878822669373367)
XLA Ops:
  0.6 54.3 %shard_map.111 = (bf16[384,512]{1,0:T(8,128)(2,1)S(1)}, bf16[384,256]{1,0:T(8,128)(2,1)S(1)}, bf16[2,4,4,16,512]{4,3,2,1,0:T(8,128)(2,1)S(1)}) custom-call(s32[16,2,16]{2,1,0:T(2,128)} %refs_0_.1, s32[16,2,16]{2,1,0:T(2,128)} %refs_1_.1, s32[16,2,16]{2,1,0:T(2,128)} %refs_2_.1, s32[96,128]{1,0:T(8,128)} %bitcast.3, bf16[3,128,256]{2,1,0:T(8,128)(2,1)} %bitcast.2, ...), custom_call_target="tpu_custom_call" | custom-call | tf_op jit(solution)/shard_map/pallas_call | solution.py:700
  55.0 1.2 %shard_map.112 = (bf16[384,512]{1,0:T(8,128)(2,1)}, bf16[384,256]{1,0:T(8,128)(2,1)}, f32[256,512]{1,0:T(8,128)}, f32[256,512]{1,0:T(8,128)}) custom-call(bf16[384,512]{1,0:T(8,128)(2,1)S(1)} %get-tuple-element.7.hidden, bf16[384,256]{1,0:T(8,128)(2,1)S(1)} %get-tuple-element.8.feat_grad, bf16[2,4,4,16,512]{4,3,2,1,0:T(8,128)(2,1)S(1)} %get-tuple-element.9.grads), custom_call_target="tpu_custom_call" | custom-call | tf_op jit(solution)/shard_map/pallas_call | solution.py:725
